TPU v7x, 32 devices: a whole 2x2x4 slice. The times are simulated.
32 devices in a mesh: dp: 4 (over x, core), vocab: 8 (over z, y).
Axes of the slice: x: 2, y: 2, z: 4, core: 2. Of those that a mesh axis runs over, the one named last changes fastest.
Arguments:
- hidden: bfloat16 [256, 3584], P('dp'), may hold values from -160 to 160
- head_weight: bfloat16 [3584, 152064], P(None, ('dp', 'vocab')), may hold values from -0.3125 to 0.3125
- teacher_ids: int32 [256, 64], P('dp'), may hold values from 0 to 152063, as said below
- teacher_probs: float32 [256, 64], P('dp'), may hold values from 0 to 0.99, as said below
- token_weight: float32 [256], P('dp'), may hold values from 4 to 32
Outputs:
- divergence: float32 [256], P('dp')
- hidden_grad: float32 [256, 3584], P('dp', 'vocab')
Inputs may be any that keep to these rules, and one draw needn't show every extreme that they name: `teacher_ids`: each row names 64 different vocabulary entries. `teacher_probs`: all positive; each row sums to between 0.5 and 0.99.
All inputs are finite; a program needn't handle non-finite values.
Results may differ from a plain program's by a relative error of at most 0.0029.
Values may be sent and summed in bfloat16 or wider, within the bound.
A program may use at most 128 MiB of HBM per device.

v0:
```python
import jax
import jax.numpy as jnp
from jax import lax
from jax.sharding import PartitionSpec as P


def body(hidden, head_weight, teacher_ids, teacher_probs, token_weight):
    tok_rows = hidden.shape[0]
    local_cols = head_weight.shape[1]
    vocab_count = lax.axis_size("vocab")
    offset = (lax.axis_index("dp") * vocab_count + lax.axis_index("vocab")) * local_cols
    logits = jnp.dot(
        lax.all_gather(hidden, "dp", axis=0, tiled=True),
        head_weight,
        preferred_element_type=jnp.float32,
    )
    all_rows = logits.shape[0]
    id_values, probs = (
        lax.all_gather(teacher_ids.astype(jnp.float32), "dp", axis=0, tiled=True),
        lax.all_gather(teacher_probs, "dp", axis=0, tiled=True),
    )
    local_ids = id_values.astype(jnp.int32) - offset
    top_count = local_ids.shape[1]
    group_size = 8
    columns = lax.broadcasted_iota(jnp.int32, (1, 1, local_cols), 2)

    def add_group(index, sparse_now):
        ids_part = lax.dynamic_slice_in_dim(local_ids, index * group_size, group_size, 1)
        probs_part = lax.dynamic_slice_in_dim(probs, index * group_size, group_size, 1)
        matches = ids_part[:, :, None] == columns
        return sparse_now + jnp.sum(jnp.where(matches, probs_part[:, :, None], 0.0), axis=1)

    sparse = lax.fori_loop(
        0, top_count // group_size, add_group, jnp.zeros((all_rows, local_cols), jnp.float32)
    )
    picked = jnp.sum(sparse * logits, axis=1)
    local_peak = jnp.max(logits, axis=1)
    largest = lax.pmax(local_peak, ("dp", "vocab"))
    local_sum = jnp.sum(jnp.exp(logits - largest[:, None]), axis=1)
    expsum, weighted = lax.psum((local_sum, picked), ("dp", "vocab"))
    log_norm = largest + jnp.log(expsum)
    mass = jnp.sum(probs, axis=1)
    divergence_all = jnp.sum(probs * jnp.log(probs), axis=1) - weighted + mass * log_norm
    divergence = lax.dynamic_slice_in_dim(
        divergence_all, lax.axis_index("dp") * tok_rows, tok_rows, 0
    )
    logit_grad = (mass[:, None] * jnp.exp(logits - log_norm[:, None]) - sparse).astype(jnp.bfloat16)
    row_sums = lax.psum_scatter(
        lax.dot_general(
            logit_grad, head_weight, (((1,), (1,)), ((), ())), preferred_element_type=jnp.float32
        ),
        "dp",
        scatter_dimension=0,
        tiled=True,
    )
    summed = lax.psum_scatter(row_sums, "vocab", scatter_dimension=1, tiled=True)
    return (divergence, token_weight[:, None] * summed)


def solution(mesh):
    in_specs = (P("dp", None), P(None, ("dp", "vocab")), P("dp", None), P("dp", None), P("dp"))
    out_specs = (P("dp"), P("dp", "vocab"))
    return jax.shard_map(body, mesh=mesh, in_specs=in_specs, out_specs=out_specs, check_vma=False)
```

profile of v0, /device:TPU:0, one launch (start us, length us, event | category | flops | bytes accessed | tf_op | source)
XLA Modules:
  0.0 376.8 jit_solution(5215880076449560533)
XLA Ops:
  8.0 6.7 %all_gather.9 = f32[256,64]{1,0:T(8,128)S(1)} all-gather(f32[64,64]{1,0:T(8,128)} %param.10), channel_id=1, replica_groups=mesh['dp'=4,'vocab'=8] {'dp'}, dimensions={0}, use_global_device_ids=true | all-gather | bytes 81920 | tf_op jit(solution)/shard_map/all_gather | solution.py:20
  15.4 5.6 %all_gather.10 = f32[256,64]{1,0:T(8,128)S(1)} all-gather(f32[64,64]{1,0:T(8,128)S(1)} %convert_element_type.9), channel_id=1, replica_groups=mesh['dp'=4,'vocab'=8] {'dp'}, dimensions={0}, use_global_device_ids=true | all-gather | bytes 81920 | tf_op jit(solution)/shard_map/all_gather | solution.py:19
  21.2 111.5 %while.14 = (s32[]{:T(128)}, f32[256,4752]{0,1:T(8,128)}, s32[256,64]{0,1:T(8,128)S(1)}, f32[256,64]{0,1:T(8,128)S(1)}, s32[]{:T(128)}, /*index=5*/s32[]{:T(128)}, s32[]{:T(128)}, s32[]{:T(128)}) while((s32[]{:T(128)}, f32[256,4752]{0,1:T(8,128)}, s32[256,64]{0,1:T(8,128)S(1)}, f32[256,64]{0,1:T(8,128)S(1)}, s32[]{:T(128)}, ...), condition=%wide.region_3.4_spmd.clone, body=%wide.region_1.3_spmd.clone.sunk | while | flops 30412804 | bytes 19513500 | solution.py:33
  21.3 7.4 %select_reduce_fusion.2 = f32[256,4752]{0,1:T(8,128)} fusion(f32[256,8]{0,1:T(8,128)S(1)} %constant_dynamic-slice_fusion.4, s32[256,8]{0,1:T(8,128)S(1)} %constant_dynamic-slice_fusion.5), kind=kLoop, calls=%fused_computation.2.clone.1 | loop fusion | flops 27979776 | bytes 4882432 | tf_op jit(solution)/shard_map/while/body/eval_jaxpr/reduce_sum | solution.py:31
  33.9 7.4 %select_reduce_fusion.2 = f32[256,4752]{0,1:T(8,128)} fusion(f32[256,8]{0,1:T(8,128)S(1)} %constant_dynamic-slice_fusion.4, s32[256,8]{0,1:T(8,128)S(1)} %constant_dynamic-slice_fusion.5), kind=kLoop, calls=%fused_computation.2.clone.1 | loop fusion | flops 27979776 | bytes 4882432 | tf_op jit(solution)/shard_map/while/body/eval_jaxpr/reduce_sum | solution.py:31
  41.3 6.7 %select_add_fusion.2 = f32[256,4752]{0,1:T(8,128)} fusion(f32[256,4752]{0,1:T(8,128)} %select_reduce_fusion.2, f32[256,4752]{0,1:T(8,128)} %get-tuple-element.170, pred[]{:T(512)S(6)} %compare.3), kind=kLoop, calls=%fused_computation.3.clone.1 | loop fusion | flops 2433024 | bytes 14598145 | tf_op jit(solution)/shard_map/while/body/eval_jaxpr/add | solution.py:31
  48.0 7.4 %select_reduce_fusion.2 = f32[256,4752]{0,1:T(8,128)} fusion(f32[256,8]{0,1:T(8,128)S(1)} %constant_dynamic-slice_fusion.4, s32[256,8]{0,1:T(8,128)S(1)} %constant_dynamic-slice_fusion.5), kind=kLoop, calls=%fused_computation.2.clone.1 | loop fusion | flops 27979776 | bytes 4882432 | tf_op jit(solution)/shard_map/while/body/eval_jaxpr/reduce_sum | solution.py:31
  55.4 6.7 %select_add_fusion.2 = f32[256,4752]{0,1:T(8,128)} fusion(f32[256,4752]{0,1:T(8,128)} %select_reduce_fusion.2, f32[256,4752]{0,1:T(8,128)} %get-tuple-element.170, pred[]{:T(512)S(6)} %compare.3), kind=kLoop, calls=%fused_computation.3.clone.1 | loop fusion | flops 2433024 | bytes 14598145 | tf_op jit(solution)/shard_map/while/body/eval_jaxpr/add | solution.py:31
  62.1 7.4 %select_reduce_fusion.2 = f32[256,4752]{0,1:T(8,128)} fusion(f32[256,8]{0,1:T(8,128)S(1)} %constant_dynamic-slice_fusion.4, s32[256,8]{0,1:T(8,128)S(1)} %constant_dynamic-slice_fusion.5), kind=kLoop, calls=%fused_computation.2.clone.1 | loop fusion | flops 27979776 | bytes 4882432 | tf_op jit(solution)/shard_map/while/body/eval_jaxpr/reduce_sum | solution.py:31
  69.5 6.7 %select_add_fusion.2 = f32[256,4752]{0,1:T(8,128)} fusion(f32[256,4752]{0,1:T(8,128)} %select_reduce_fusion.2, f32[256,4752]{0,1:T(8,128)} %get-tuple-element.170, pred[]{:T(512)S(6)} %compare.3), kind=kLoop, calls=%fused_computation.3.clone.1 | loop fusion | flops 2433024 | bytes 14598145 | tf_op jit(solution)/shard_map/while/body/eval_jaxpr/add | solution.py:31
  76.2 7.4 %select_reduce_fusion.2 = f32[256,4752]{0,1:T(8,128)} fusion(f32[256,8]{0,1:T(8,128)S(1)} %constant_dynamic-slice_fusion.4, s32[256,8]{0,1:T(8,128)S(1)} %constant_dynamic-slice_fusion.5), kind=kLoop, calls=%fused_computation.2.clone.1 | loop fusion | flops 27979776 | bytes 4882432 | tf_op jit(solution)/shard_map/while/body/eval_jaxpr/reduce_sum | solution.py:31
  83.6 6.7 %select_add_fusion.2 = f32[256,4752]{0,1:T(8,128)} fusion(f32[256,4752]{0,1:T(8,128)} %select_reduce_fusion.2, f32[256,4752]{0,1:T(8,128)} %get-tuple-element.170, pred[]{:T(512)S(6)} %compare.3), kind=kLoop, calls=%fused_computation.3.clone.1 | loop fusion | flops 2433024 | bytes 14598145 | tf_op jit(solution)/shard_map/while/body/eval_jaxpr/add | solution.py:31
  90.3 7.4 %select_reduce_fusion.2 = f32[256,4752]{0,1:T(8,128)} fusion(f32[256,8]{0,1:T(8,128)S(1)} %constant_dynamic-slice_fusion.4, s32[256,8]{0,1:T(8,128)S(1)} %constant_dynamic-slice_fusion.5), kind=kLoop, calls=%fused_computation.2.clone.1 | loop fusion | flops 27979776 | bytes 4882432 | tf_op jit(solution)/shard_map/while/body/eval_jaxpr/reduce_sum | solution.py:31
  97.8 6.7 %select_add_fusion.2 = f32[256,4752]{0,1:T(8,128)} fusion(f32[256,4752]{0,1:T(8,128)} %select_reduce_fusion.2, f32[256,4752]{0,1:T(8,128)} %get-tuple-element.170, pred[]{:T(512)S(6)} %compare.3), kind=kLoop, calls=%fused_computation.3.clone.1 | loop fusion | flops 2433024 | bytes 14598145 | tf_op jit(solution)/shard_map/while/body/eval_jaxpr/add | solution.py:31
  104.5 7.4 %select_reduce_fusion.2 = f32[256,4752]{0,1:T(8,128)} fusion(f32[256,8]{0,1:T(8,128)S(1)} %constant_dynamic-slice_fusion.4, s32[256,8]{0,1:T(8,128)S(1)} %constant_dynamic-slice_fusion.5), kind=kLoop, calls=%fused_computation.2.clone.1 | loop fusion | flops 27979776 | bytes 4882432 | tf_op jit(solution)/shard_map/while/body/eval_jaxpr/reduce_sum | solution.py:31
  111.9 6.7 %select_add_fusion.2 = f32[256,4752]{0,1:T(8,128)} fusion(f32[256,4752]{0,1:T(8,128)} %select_reduce_fusion.2, f32[256,4752]{0,1:T(8,128)} %get-tuple-element.170, pred[]{:T(512)S(6)} %compare.3), kind=kLoop, calls=%fused_computation.3.clone.1 | loop fusion | flops 2433024 | bytes 14598145 | tf_op jit(solution)/shard_map/while/body/eval_jaxpr/add | solution.py:31
  118.6 7.4 %select_reduce_fusion.2 = f32[256,4752]{0,1:T(8,128)} fusion(f32[256,8]{0,1:T(8,128)S(1)} %constant_dynamic-slice_fusion.4, s32[256,8]{0,1:T(8,128)S(1)} %constant_dynamic-slice_fusion.5), kind=kLoop, calls=%fused_computation.2.clone.1 | loop fusion | flops 27979776 | bytes 4882432 | tf_op jit(solution)/shard_map/while/body/eval_jaxpr/reduce_sum | solution.py:31
  126.0 6.7 %select_add_fusion.2 = f32[256,4752]{0,1:T(8,128)} fusion(f32[256,4752]{0,1:T(8,128)} %select_reduce_fusion.2, f32[256,4752]{0,1:T(8,128)} %get-tuple-element.170, pred[]{:T(512)S(6)} %compare.3), kind=kLoop, calls=%fused_computation.3.clone.1 | loop fusion | flops 2433024 | bytes 14598145 | tf_op jit(solution)/shard_map/while/body/eval_jaxpr/add | solution.py:31
  132.8 17.7 %fusion.6 = (f32[256]{0:T(256)S(1)}, f32[256,4752]{0,1:T(8,128)}) fusion(bf16[256,3584]{1,0:T(8,128)(2,1)} %all-gather.2.cloned.1.call-done, bf16[3584,4752]{0,1:T(8,128)(2,1)} %param.8), kind=kOutput, calls=%fused_computation.18 | convolution fusion | flops 8721174528 | bytes 40764416 | tf_op jit(solution)/shard_map/dot_general | solution.py:12
  150.5 40.7 %pmax.7 = f32[256]{0:T(256)S(1)} all-reduce(f32[256]{0:T(256)S(1)} %get-tuple-element.134), channel_id=1, replica_groups=mesh['dp'=4,'vocab'=8] {'dp','vocab'}, use_global_device_ids=true, to_apply=%region_8.9 | all-reduce | flops 256 | bytes 2048 | tf_op jit(solution)/shard_map/pmax | solution.py:38
  196.1 40.2 %all-reduce = (f32[256]{0:T(256)S(1)}, f32[256]{0:T(256)S(1)}) all-reduce(f32[256]{0:T(256)S(1)} %get-tuple-element.119, f32[256]{0:T(256)S(1)} %get-tuple-element.118), channel_id=1, replica_groups=mesh['dp'=4,'vocab'=8] {'dp','vocab'}, use_global_device_ids=true, to_apply=%region_10.11 | all-reduce | flops 512 | bytes 4096 | tf_op jit(solution)/shard_map/psum | solution.py:40
  236.3 19.5 %fusion.2 = f32[256,3584]{1,0:T(8,128)} fusion(bf16[3584,4752]{0,1:T(8,128)(2,1)} %param.8, f32[256,4752]{0,1:T(8,128)} %get-tuple-element.96, f32[256,4752]{0,1:T(8,128)} %get-tuple-element.135, f32[256]{0:T(256)S(1)} %get-tuple-element.133, f32[256]{0:T(256)S(1)} %get-tuple-element.121), kind=kOutput, calls=%fused_computation.9 | convolution fusion | flops 8724824064 | bytes 47466496 | tf_op jit(solution)/shard_map/dot_general | solution.py:49
  255.9 42.0 %reduce-scatter.5.cloned.1.call-done = f32[64,3584]{1,0:T(8,128)} async-done(((f32[256,3584]{1,0:T(8,128)}), f32[64,3584]{1,0:T(8,128)}) %reduce-scatter.5.cloned.1.call-update) | async-done | bytes 917520 | tf_op jit(solution)/shard_map/reduce_scatter | solution.py:48
  301.5 67.0 %reduce-scatter.7.cloned.1.call-done = f32[448,64]{1,0:T(8,128)} async-done(((f32[3584,64]{1,0:T(8,128)}), f32[448,64]{1,0:T(8,128)}) %reduce-scatter.7.cloned.1.call-update) | async-done | bytes 114704
  (38 shorter events, 17.5 us)
Async XLA Ops:
  7.2 125.7 %all-gather.2.cloned.1.call-start = ((), (), s32[]{:S(2)}) async-start(), calls=%async_computation.2 | async-start | bytes 2293760 | tf_op jit(solution)/shard_map/all_gather | solution.py:13
  7.9 290.0 %reduce-scatter.5.cloned.1.call-start = ((), (), s32[]{:S(2)}) async-start(), calls=%async_computation.3 | async-start | bytes 4587520 | tf_op jit(solution)/shard_map/reduce_scatter | solution.py:48
  255.8 113.8 %copy-start = (f32[64]{0:T(128)S(1)}, f32[64]{0:T(128)}, u32[]{:S(2)}) copy-start(f32[64]{0:T(128)} %param.11) | copy-start | bytes 772
  255.8 112.7 %reduce-scatter.7.cloned.1.call-start = ((), (), s32[]{:S(2)}) async-start(), calls=%async_computation.4 | async-start | bytes 2064384
Sparse Core Ops, SparseCore 0:
  9.5 23.8 all-gather.1
  255.9 41.9 reduce-scatter.4
  301.4 67.0 reduce-scatter.6
where the time goes:
time: 377 us
  other arithmetic  118 us (31%)
  waiting for transfers between devices  110 us (29%)
  blocking collectives  93.2 us (25%)
  matrix products  37.2 us (10%)
  between operations  13.8 us (4%)
  local copies, waits for them, and re-layouts  4.81 us (1%)
    unnamed x4, waiting for transfers between devices  67.7 us
    reduce_sum x8, other arithmetic, add_group(): jnp.sum(jnp.where(matches, probs_part[:, :, None], 0.0), axis=1)  59.2 us
    add x8, other arithmetic, add_group(): sparse_now + jnp.sum(jnp.where(matches, probs_part[:, :, None], 0.0), axi...  52.1 us
    reduce_scatter x1, waiting for transfers between devices, body(): lax.psum_scatter(lax.dot_general(logit_grad, head_weight, (((1,), (1,)),...  42 us
    pmax x1, blocking collectives, body(): largest = lax.pmax(local_peak, ('dp', 'vocab'))  40.7 us
    psum x1, blocking collectives, body(): expsum, weighted = lax.psum((local_sum, picked), ('dp', 'vocab'))  40.2 us
    dot_general x1, matrix products, body(): lax.dot_general(logit_grad, head_weight, (((1,), (1,)), ((), ())), prefer...  19.5 us
    dot_general x1, matrix products, body(): jnp.dot(lax.all_gather(hidden, 'dp', axis=0, tiled=True), head_weight, pr...  17.7 us
  transfers between devices with their start and end apart: 3, of which 2 were waited for; matrix products, arithmetic and copies ran while one was open for 30% of the time, Pallas kernels for 0%

commit v1 on v0

v1 whole, which is shorter than its diff:
```python
import functools

import jax
import jax.numpy as jnp
from jax import lax
from jax.experimental import pallas as pl
from jax.experimental.pallas import tpu as pltpu
from jax.sharding import PartitionSpec as P

MESH = pl.DeviceIdType.MESH
NT = (((1,), (1,)), ((), ()))


def windows(feat):
    q = next(k for k in (1, 2, 4, 8, 16, 32, 64, 128) if k * feat % 128 == 0)
    first = [m * feat // 128 * 128 for m in range(q)]
    ww = max((m + 1) * feat - first[m] + 127 for m in range(q)) // 128 * 128
    return q, ww, [min(f, q * feat - ww) for f in first]


def kernel(
    ndp, nv, kc, hid, w, tp, tw, div_out, grad_out,
    wv, h_all, tp_all, sp, logits, lg, g, r1, s2, r2, stats, cols, cols2, back, own,
    w_sem, l_sem, hx_s, hx_r, hc_s, hc_r, tp_s, tp_r, st_s, st_r, g1_s, g1_r, g2_s, g2_r,
):
    d, mv = lax.axis_index("dp"), lax.axis_index("vocab")
    x, core = d // 2, d % 2
    nx, nd = ndp // 2, ndp * nv
    me = d * nv + mv
    rows, depth = hid.shape
    cols_n = w.shape[0]
    tok = rows * ndp
    nk = depth // kc
    nt = (cols_n + 127) // 128
    feat = depth // nv
    q, ww, starts = windows(feat)
    ng, group = nv // q, q * feat
    mg, mm = mv // q, lax.rem(mv, q)
    other = (2 * x + 1 - core, mv)

    def block(dp_index):
        return pl.ds(pl.multiple_of(dp_index * rows, rows), rows)

    def w_copy(c):
        part = pl.ds(pl.multiple_of(c * kc, kc), kc)
        return pltpu.make_async_copy(w.at[:, part], wv.at[:, part], w_sem.at[c])

    def l_copy():
        return pltpu.make_async_copy(hid, h_all.at[block(d), :], l_sem.at[0])

    def kpart(c):
        return pl.ds(pl.multiple_of(c * kc, kc), kc)

    def hx_copy(j, c):
        return pltpu.make_async_remote_copy(
            src_ref=hid.at[:, kpart(c)], dst_ref=h_all.at[block(d), kpart(c)],
            send_sem=hx_s.at[j - 1, c], recv_sem=hx_r.at[j - 1, c],
            device_id=(2 * lax.rem(x + j, nx) + core, mv), device_id_type=MESH)

    def hx_in(j, c):
        src = block(2 * lax.rem(x + nx - j, nx) + core)
        return pltpu.make_async_remote_copy(
            src_ref=h_all.at[src, kpart(c)], dst_ref=h_all.at[src, kpart(c)],
            send_sem=hx_s.at[j - 1, c], recv_sem=hx_r.at[j - 1, c],
            device_id=other, device_id_type=MESH)

    def hc_copy(j, c):
        if j == 0:
            src = hid.at[:, kpart(c)]
        else:
            src = h_all.at[block(2 * lax.rem(x + nx - j, nx) + core), kpart(c)]
        return pltpu.make_async_remote_copy(
            src_ref=src,
            dst_ref=h_all.at[block(2 * lax.rem(x + nx - j, nx) + core), kpart(c)],
            send_sem=hc_s.at[j, c], recv_sem=hc_r.at[j, c],
            device_id=other, device_id_type=MESH)

    def hc_in(j, c):
        dst = h_all.at[block(2 * lax.rem(x + nx - j, nx) + 1 - core), kpart(c)]
        return pltpu.make_async_remote_copy(
            src_ref=dst, dst_ref=dst, send_sem=hc_s.at[j, c], recv_sem=hc_r.at[j, c],
            device_id=other, device_id_type=MESH)

    def tp_copy(j, sender):
        return pltpu.make_async_remote_copy(
            src_ref=tp if sender is d else tp_all.at[block(sender), :],
            dst_ref=tp_all.at[block(sender), :],
            send_sem=tp_s.at[j - 1], recv_sem=tp_r.at[j - 1],
            device_id=(lax.rem(d + j, ndp), mv), device_id_type=MESH)

    def st_copy(j, sender):
        to = lax.rem(me + j, nd)
        return pltpu.make_async_remote_copy(
            src_ref=stats.at[sender], dst_ref=stats.at[sender],
            send_sem=st_s.at[j - 1], recv_sem=st_r.at[j - 1],
            device_id=(to // nv, lax.rem(to, nv)), device_id_type=MESH)

    def g1_copy(i, jx):
        theirs = block(2 * lax.rem(x + jx, nx) + 1 - core)
        return pltpu.make_async_remote_copy(
            src_ref=g.at[i, theirs, :], dst_ref=r1.at[i, jx],
            send_sem=g1_s.at[i, jx], recv_sem=g1_r.at[i, jx],
            device_id=other, device_id_type=MESH)

    def g2_copy(i, m, jx):
        return pltpu.make_async_remote_copy(
            src_ref=s2.at[i, m, jx], dst_ref=r2.at[i, mm, jx],
            send_sem=g2_s.at[i, m, jx], recv_sem=g2_r.at[i, mm, jx],
            device_id=(2 * lax.rem(x + jx, nx) + core, lax.rem(mg + 1 + i, ng) * q + m),
            device_id_type=MESH)

    def g2_in(i, m, jx):
        return pltpu.make_async_remote_copy(
            src_ref=r2.at[i, m, jx], dst_ref=r2.at[i, m, jx],
            send_sem=g2_s.at[i, m, jx], recv_sem=g2_r.at[i, m, jx],
            device_id=other, device_id_type=MESH)

    for c in range(nk):
        w_copy(c).start()
    l_copy().start()

    barrier = pltpu.get_barrier_semaphore()

    def greet(j, _):
        to = lax.rem(me + j, nd)
        pl.semaphore_signal(
            barrier, inc=1, device_id=(to // nv, lax.rem(to, nv)), device_id_type=MESH)
        return 0

    lax.fori_loop(1, nd, greet, 0)
    pl.semaphore_wait(barrier, nd - 1)

    for j in range(1, ndp):
        tp_copy(j, d).start()
    for c in range(nk):
        for j in range(1, nx):
            hx_copy(j, c).start()
        hc_copy(0, c).start()

    tp_all[block(d), :] = tp[...]
    for a in range(nt):
        logits[:, a * 128:(a + 1) * 128] = jnp.zeros((tok, 128), jnp.float32)
    if cols_n % 128:
        lane = lax.broadcasted_iota(jnp.int32, (tok, 128), 1)
        logits[:, (nt - 1) * 128:] = jnp.where(lane < cols_n % 128, 0.0, -1e30)
    for j in range(1, ndp):
        tp_copy(j, lax.rem(d + ndp - j, ndp)).wait_recv()

    offset = (me * cols_n).astype(jnp.float32)
    na = sp.shape[0] // tok
    iota_a = lax.broadcasted_iota(jnp.int32, (na, 128), 0)
    iota_b = lax.broadcasted_iota(jnp.int32, (128, 128), 0)
    lane8 = lax.broadcasted_iota(jnp.int32, (8, 128), 1)

    def build(step, _):
        t0 = pl.multiple_of(step * 8, 8)
        both = tp_all[pl.ds(t0, 8), :]
        turned = pltpu.roll(both, 64, 1)
        ids = jnp.where(lane8 < 64, both, turned)
        probs = jnp.where(lane8 < 64, turned, both)
        high = probs.astype(jnp.bfloat16).astype(jnp.float32)
        parts = jnp.where(lane8 < 64, high, probs - high)
        local = (ids - offset).astype(jnp.int32)
        inside = (local >= 0) & (local < cols_n)
        tile = jnp.where(inside, local >> 7, -1)
        low = local & 127
        for r in range(8):
            left = jnp.where(iota_a == tile[r:r + 1, :], parts[r:r + 1, :], 0.0)
            right = jnp.where(iota_b == low[r:r + 1, :], 1.0, 0.0)
            sp[pl.ds(t0 + r, na, stride=tok), :] = lax.dot_general(
                left.astype(jnp.bfloat16), right.astype(jnp.bfloat16), NT,
                preferred_element_type=jnp.float32)
        return 0

    lax.fori_loop(0, tok // 8, build, 0)

    def forward_in(c):
        for j in range(1, nx):
            hx_in(j, c).wait_recv()
            hc_copy(j, c).start()

    l_copy().wait()
    forward_in(0)
    wide = 512

    def first(c, _):
        @pl.when(c + 1 < nk)
        def _():
            forward_in(c + 1)

        for j in range(nx):
            hc_in(j, c).wait_recv()
        w_copy(c).wait()
        hc = h_all[:, kpart(c)]
        for n0 in range(0, cols_n, wide):
            n1 = min(n0 + wide, cols_n)
            logits[:, n0:n1] += lax.dot_general(
                hc, wv[n0:n1, kpart(c)], NT, preferred_element_type=jnp.float32)
        return 0

    lax.fori_loop(0, nk, first, 0)

    def peak(step, _):
        t0 = pl.multiple_of(step * 8, 8)
        ts = pl.ds(t0, 8)
        vals = [logits[ts, a * 128:(a + 1) * 128] for a in range(nt)]
        top = functools.reduce(jnp.maximum, vals)
        m = jnp.max(top, axis=1, keepdims=True)
        total = jnp.zeros((8, 128), jnp.float32)
        picked = jnp.zeros((8, 128), jnp.float32)
        for a in range(nt):
            picked += vals[a] * sp[pl.ds(a * tok + t0, 8), :]
            e = jnp.exp(vals[a] - m)
            logits[ts, a * 128:(a + 1) * 128] = e
            total += e
        s = jnp.sum(total, axis=1, keepdims=True)
        q = jnp.sum(picked, axis=1, keepdims=True)
        cols[ts, :] = jnp.where(lane8 == 0, m, jnp.where(lane8 == 1, s, q))
        return 0

    lax.fori_loop(0, tok // 8, peak, 0, unroll=2)

    turned_stats = cols[...].T
    for j in range(tok // 128):
        stats[me, 3 * j:3 * j + 3, :] = turned_stats[0:3, j * 128:(j + 1) * 128]
    for j in range(1, nd):
        st_copy(j, me).start()
    back[...] = jnp.zeros_like(back)
    for j in range(1, nd):
        st_copy(j, lax.rem(me + nd - j, nd)).wait_recv()
    for j in range(tok // 128):
        part = slice(j * 128, (j + 1) * 128)
        ms = stats[:, 3 * j, :]
        big = jnp.max(ms, axis=0, keepdims=True)
        z = jnp.sum(stats[:, 3 * j + 1, :] * jnp.exp(ms - big), axis=0, keepdims=True)
        back[0:1, part] = big + jnp.log(z)
        back[1:2, part] = jnp.sum(stats[:, 3 * j + 2, :], axis=0, keepdims=True)
    cols2[...] = back[...].T

    lane16 = lax.broadcasted_iota(jnp.int32, (16, 128), 1)

    def grad(step, _):
        t0 = pl.multiple_of(step * 16, 16)
        ts = pl.ds(t0, 16)
        mass = jnp.sum(jnp.where(lane16 >= 64, tp_all[ts, :], 0.0), axis=1, keepdims=True)
        scale = mass * jnp.exp(cols[ts, 0:1] - cols2[ts, 0:1])
        for a in range(nt):
            n1 = min(128, cols_n - a * 128)
            value = logits[ts, a * 128:(a + 1) * 128] * scale - sp[pl.ds(a * tok + t0, 16), :]
            lg[ts, a * 128:a * 128 + n1] = value[:, :n1].astype(jnp.bfloat16)
        return 0

    lax.fori_loop(0, tok // 16, grad, 0, unroll=2)

    def send_block(i, m, jx, both):
        s2[i, m, jx] = both[:, starts[m]:starts[m] + ww].astype(jnp.bfloat16)
        g2_copy(i, m, jx).start()

    def pass_on(i, last):
        for jx in range(nx):
            g1_copy(i, jx).wait_recv()
            mine = block(2 * lax.rem(x + jx, nx) + core)
            both = g[i, mine, :] + r1[i, jx]
            for m in range(q):
                if last and jx == 0:
                    @pl.when(m == mm)
                    def _():
                        own[...] = both[:, starts[m]:starts[m] + ww]

                    @pl.when(m != mm)
                    def _():
                        send_block(i, m, jx, both)
                else:
                    send_block(i, m, jx, both)

    def second(i, _):
        part = pl.ds(pl.multiple_of(lax.rem(mg + 1 + i, ng) * group, group), group)
        g[i] = jnp.dot(lg[...], wv[:, part], preferred_element_type=jnp.float32)
        for jx in range(nx):
            g1_copy(i, jx).start()

        @pl.when(i > 0)
        def _():
            pass_on(i - 1, False)

        return 0

    lax.fori_loop(0, ng, second, 0)
    pass_on(ng - 1, True)

    def not_own(i, m, jx):
        return (m != mm) if (i == ng - 1 and jx == 0) else (mm >= 0)

    mine = block(d)
    lane = lax.broadcasted_iota(jnp.int32, (rows, 128), 1)
    probs = jnp.where(lane >= 64, tp_all[mine, :], 1.0)
    entropy = jnp.sum(probs * jnp.log(probs), axis=1, keepdims=True)
    mass = jnp.sum(jnp.where(lane >= 64, probs, 0.0), axis=1, keepdims=True)
    div_out[...] = entropy - cols2[mine, 1:2] + mass * cols2[mine, 0:1]

    for i in range(ng):
        for jx in range(nx):
            for m in range(q):
                @pl.when(not_own(i, m, jx))
                def _():
                    g2_in(i, m, jx).wait_recv()
                    own[...] += r2[i, m, jx].astype(jnp.float32)
    for m in range(q):
        @pl.when(m == mm)
        def _():
            lo = m * feat - starts[m]
            grad_out[...] = own[:, lo:lo + feat] * tw[...]

    for c in range(nk):
        for j in range(1, nx):
            hx_copy(j, c).wait_send()
        for j in range(nx):
            hc_copy(j, c).wait_send()
    for j in range(1, ndp):
        tp_copy(j, d).wait_send()
    for j in range(1, nd):
        st_copy(j, me).wait_send()
    for i in range(ng):
        for jx in range(nx):
            g1_copy(i, jx).wait_send()
            for m in range(q):
                @pl.when(not_own(i, m, jx))
                def _():
                    g2_copy(i, m, jx).wait_send()


def body(ndp, nv, hidden, head_weight, teacher_ids, teacher_probs, token_weight):
    rows, depth = hidden.shape
    cols_n = head_weight.shape[1]
    tok, nx, nd, feat = rows * ndp, ndp // 2, ndp * nv, depth // nv
    q, ww, _ = windows(feat)
    ng, group = nv // q, q * feat
    kc = next(k for k in (512, 256, 128) if depth % k == 0)
    nk = depth // kc
    nt = (cols_n + 127) // 128
    na = (nt + 7) // 8 * 8
    srows = (3 * (tok // 128) + 7) // 8 * 8
    tp = jnp.concatenate([teacher_ids.astype(jnp.float32), teacher_probs], axis=1)
    f32, bf16, dma = jnp.float32, jnp.bfloat16, pltpu.SemaphoreType.DMA
    anyspace = pl.BlockSpec(memory_space=pl.ANY)
    vmem = pl.BlockSpec(memory_space=pltpu.VMEM)
    div, out = pl.pallas_call(
        functools.partial(kernel, ndp, nv, kc),
        out_shape=(
            jax.ShapeDtypeStruct((rows, 1), f32), jax.ShapeDtypeStruct((rows, feat), f32)),
        in_specs=[anyspace, anyspace, vmem, vmem],
        out_specs=(vmem, vmem),
        scratch_shapes=[
            pltpu.VMEM((cols_n, depth), bf16), pltpu.VMEM((tok, depth), bf16),
            pltpu.VMEM((tok, 128), f32), pltpu.VMEM((na * tok, 128), f32),
            pltpu.VMEM((tok, nt * 128), f32), pltpu.VMEM((tok, cols_n), bf16),
            pltpu.VMEM((ng, tok, group), f32), pltpu.VMEM((ng, nx, rows, group), f32),
            pltpu.VMEM((ng, q, nx, rows, ww), bf16), pltpu.VMEM((ng, q, nx, rows, ww), bf16),
            pltpu.VMEM((nd, srows, 128), f32), pltpu.VMEM((tok, 128), f32),
            pltpu.VMEM((tok, 128), f32), pltpu.VMEM((128, tok), f32),
            pltpu.VMEM((rows, ww), f32),
            dma((nk,)), dma((1,)), dma((nx - 1, nk)), dma((nx - 1, nk)),
            dma((nx, nk)), dma((nx, nk)), dma((ndp - 1,)), dma((ndp - 1,)),
            dma((nd - 1,)), dma((nd - 1,)), dma((ng, nx)), dma((ng, nx)),
            dma((ng, q, nx)), dma((ng, q, nx)),
        ],
        compiler_params=pltpu.CompilerParams(
            collective_id=0, has_side_effects=True, vmem_limit_bytes=67043328),
    )(hidden, head_weight.T, tp, token_weight[:, None])
    return div[:, 0], out


def solution(mesh):
    in_specs = (P("dp", None), P(None, ("dp", "vocab")), P("dp", None), P("dp", None), P("dp"))
    out_specs = (P("dp"), P("dp", "vocab"))
    return jax.shard_map(
        functools.partial(body, mesh.shape["dp"], mesh.shape["vocab"]),
        mesh=mesh, in_specs=in_specs, out_specs=out_specs, check_vma=False)
```

time: 377 us -> 87.3 us (0.23)
  the two profiles are of different devices: /device:TPU:0 before, /device:TPU:13 now
where the time goes in v1:
time: 87.3 us; the launch traced here: 86.9 us
  Pallas kernels  79.7 us (91%)
  other arithmetic  3.6 us (4%)
  local copies, waits for them, and re-layouts  2.91 us (3%)
    pallas_call x1, Pallas kernels, body(): pl.pallas_call(functools.partial(kernel, ndp, nv, kc), out_shape=(jax.Sha...  79.7 us

profile of v1, /device:TPU:13, one launch (start us, length us, event | category | flops | bytes accessed | tf_op | source)
XLA Modules:
  0.0 86.9 jit_solution(8512543166762708367)
XLA Ops:
  0.6 0.8 convert_element_type.3
  1.4 1.5 %pad_maximum_fusion.tp = f32[64,128]{1,0:T(8,128)} fusion(f32[64,64]{1,0:T(8,128)} %param.8, f32[64,64]{1,0:T(8,128)S(1)} %convert_element_type.3), kind=kLoop, calls=%fused_computation | loop fusion | flops 8192 | bytes 65536 | tf_op jit(solution)/shard_map/concatenate | solution.py:343
  2.8 1.3 %copy.8.tw = f32[64,1]{1,0:T(8,128)} copy(f32[64,1]{0,1:T(1,128)} %bitcast.3) | data formatting | bytes 512 | tf_op jit(solution)/shard_map/broadcast_in_dim | solution.py:369
  4.2 79.7 %shard_map.68 = (f32[64,1]{1,0:T(8,128)}, f32[64,448]{1,0:T(8,128)}) custom-call(bf16[64,3584]{1,0:T(8,128)(2,1)} %hid.1, bf16[4752,3584]{1,0:T(8,128)(2,1)} %bitcast.2, f32[64,128]{1,0:T(8,128)} %pad_maximum_fusion.tp, f32[64,1]{1,0:T(8,128)} %copy.8.tw), custom_call_target="tpu_custom_call" | custom-call | tf_op jit(solution)/shard_map/pallas_call | solution.py:347
  83.9 1.4 %reduce = f32[64]{0:T(128)} reduce(f32[64,1]{1,0:T(8,128)} %get-tuple-element.4, f32[]{:T(128)} %constant.1), dimensions={1}, to_apply=%get-tuple-element.4.reduce_sub_computation | reduce | bytes 516 | tf_op jit(solution)/shard_map/pallas_call | solution.py:347
  85.3 1.6 %copy.10 = f32[64,448]{1,0:T(8,128)} copy(f32[64,448]{1,0:T(8,128)} %get-tuple-element.9) | data formatting | bytes 229376

commit v2 on v1

--- a/solution.py
+++ b/solution.py
@@ -19,9 +19,9 @@
 
 
 def kernel(
-    ndp, nv, kc, hid, w, tp, tw, div_out, grad_out,
-    wv, h_all, tp_all, sp, logits, lg, g, r1, s2, r2, stats, cols, cols2, back, own,
-    w_sem, l_sem, hx_s, hx_r, hc_s, hc_r, tp_s, tp_r, st_s, st_r, g1_s, g1_r, g2_s, g2_r,
+    ndp, nv, kc, hid, w, ids_in, probs_in, tw, div_out, grad_out,
+    wv, h_all, tp_all, sp, logits, lg, g, r1, sx, rx, s2, r2, stats, cols, cols2, back, own,
+    w_sem, l_sem, hx_s, hx_r, hc_s, hc_r, tp_s, tp_r, st_s, st_r, g1_s, g1_r, gx_s, gx_r, g2_s, g2_r,
 ):
     d, mv = lax.axis_index("dp"), lax.axis_index("vocab")
     x, core = d // 2, d % 2
@@ -83,7 +83,7 @@
 
     def tp_copy(j, sender):
         return pltpu.make_async_remote_copy(
-            src_ref=tp if sender is d else tp_all.at[block(sender), :],
+            src_ref=tp_all.at[block(sender), :],
             dst_ref=tp_all.at[block(sender), :],
             send_sem=tp_s.at[j - 1], recv_sem=tp_r.at[j - 1],
             device_id=(lax.rem(d + j, ndp), mv), device_id_type=MESH)
@@ -102,22 +102,31 @@
             send_sem=g1_s.at[i, jx], recv_sem=g1_r.at[i, jx],
             device_id=other, device_id_type=MESH)
 
-    def g2_copy(i, m, jx):
-        return pltpu.make_async_remote_copy(
-            src_ref=s2.at[i, m, jx], dst_ref=r2.at[i, mm, jx],
-            send_sem=g2_s.at[i, m, jx], recv_sem=g2_r.at[i, mm, jx],
-            device_id=(2 * lax.rem(x + jx, nx) + core, lax.rem(mg + 1 + i, ng) * q + m),
-            device_id_type=MESH)
-
-    def g2_in(i, m, jx):
-        return pltpu.make_async_remote_copy(
-            src_ref=r2.at[i, m, jx], dst_ref=r2.at[i, m, jx],
-            send_sem=g2_s.at[i, m, jx], recv_sem=g2_r.at[i, m, jx],
+    def gx_copy(i, jx):
+        return pltpu.make_async_remote_copy(
+            src_ref=sx.at[i, jx - 1], dst_ref=rx.at[i, jx - 1],
+            send_sem=gx_s.at[i, jx - 1], recv_sem=gx_r.at[i, jx - 1],
+            device_id=(2 * lax.rem(x + jx, nx) + core, mv), device_id_type=MESH)
+
+    def g2_copy(i, m):
+        return pltpu.make_async_remote_copy(
+            src_ref=s2.at[i, m], dst_ref=r2.at[i, mm],
+            send_sem=g2_s.at[i, m], recv_sem=g2_r.at[i, mm],
+            device_id=(d, lax.rem(mg + 1 + i, ng) * q + m), device_id_type=MESH)
+
+    def g2_in(i, m):
+        return pltpu.make_async_remote_copy(
+            src_ref=r2.at[i, m], dst_ref=r2.at[i, m],
+            send_sem=g2_s.at[i, m], recv_sem=g2_r.at[i, m],
             device_id=other, device_id_type=MESH)
 
     for c in range(nk):
         w_copy(c).start()
     l_copy().start()
+
+    top_n = ids_in.shape[1]
+    tp_all[block(d), 0:top_n] = ids_in[...].astype(jnp.float32)
+    tp_all[block(d), top_n:2 * top_n] = probs_in[...]
 
     barrier = pltpu.get_barrier_semaphore()
 
@@ -137,7 +146,6 @@
             hx_copy(j, c).start()
         hc_copy(0, c).start()
 
-    tp_all[block(d), :] = tp[...]
     for a in range(nt):
         logits[:, a * 128:(a + 1) * 128] = jnp.zeros((tok, 128), jnp.float32)
     if cols_n % 128:
@@ -155,11 +163,11 @@
     def build(step, _):
         t0 = pl.multiple_of(step * 8, 8)
         both = tp_all[pl.ds(t0, 8), :]
-        turned = pltpu.roll(both, 64, 1)
-        ids = jnp.where(lane8 < 64, both, turned)
-        probs = jnp.where(lane8 < 64, turned, both)
+        turned = pltpu.roll(both, top_n, 1)
+        ids = jnp.where(lane8 < top_n, both, turned)
+        probs = jnp.where(lane8 < top_n, turned, both)
         high = probs.astype(jnp.bfloat16).astype(jnp.float32)
-        parts = jnp.where(lane8 < 64, high, probs - high)
+        parts = jnp.where(lane8 < top_n, high, probs - high)
         local = (ids - offset).astype(jnp.int32)
         inside = (local >= 0) & (local < cols_n)
         tile = jnp.where(inside, local >> 7, -1)
@@ -200,25 +208,30 @@
 
     lax.fori_loop(0, nk, first, 0)
 
+    deep = 32
+    lane_deep = lax.broadcasted_iota(jnp.int32, (deep, 128), 1)
+
     def peak(step, _):
-        t0 = pl.multiple_of(step * 8, 8)
-        ts = pl.ds(t0, 8)
-        vals = [logits[ts, a * 128:(a + 1) * 128] for a in range(nt)]
-        top = functools.reduce(jnp.maximum, vals)
+        t0 = pl.multiple_of(step * deep, deep)
+        ts = pl.ds(t0, deep)
+        top = logits[ts, 0:128]
+        for a in range(1, nt):
+            top = jnp.maximum(top, logits[ts, a * 128:(a + 1) * 128])
         m = jnp.max(top, axis=1, keepdims=True)
-        total = jnp.zeros((8, 128), jnp.float32)
-        picked = jnp.zeros((8, 128), jnp.float32)
+        total = jnp.zeros((deep, 128), jnp.float32)
+        picked = jnp.zeros((deep, 128), jnp.float32)
         for a in range(nt):
-            picked += vals[a] * sp[pl.ds(a * tok + t0, 8), :]
-            e = jnp.exp(vals[a] - m)
+            value = logits[ts, a * 128:(a + 1) * 128]
+            picked += value * sp[pl.ds(a * tok + t0, deep), :]
+            e = jnp.exp(value - m)
             logits[ts, a * 128:(a + 1) * 128] = e
             total += e
         s = jnp.sum(total, axis=1, keepdims=True)
         q = jnp.sum(picked, axis=1, keepdims=True)
-        cols[ts, :] = jnp.where(lane8 == 0, m, jnp.where(lane8 == 1, s, q))
-        return 0
-
-    lax.fori_loop(0, tok // 8, peak, 0, unroll=2)
+        cols[ts, :] = jnp.where(lane_deep == 0, m, jnp.where(lane_deep == 1, s, q))
+        return 0
+
+    lax.fori_loop(0, tok // deep, peak, 0)
 
     turned_stats = cols[...].T
     for j in range(tok // 128):
@@ -242,7 +255,7 @@
     def grad(step, _):
         t0 = pl.multiple_of(step * 16, 16)
         ts = pl.ds(t0, 16)
-        mass = jnp.sum(jnp.where(lane16 >= 64, tp_all[ts, :], 0.0), axis=1, keepdims=True)
+        mass = jnp.sum(jnp.where(lane16 >= top_n, tp_all[ts, :], 0.0), axis=1, keepdims=True)
         scale = mass * jnp.exp(cols[ts, 0:1] - cols2[ts, 0:1])
         for a in range(nt):
             n1 = min(128, cols_n - a * 128)
@@ -252,26 +265,33 @@
 
     lax.fori_loop(0, tok // 16, grad, 0, unroll=2)
 
-    def send_block(i, m, jx, both):
-        s2[i, m, jx] = both[:, starts[m]:starts[m] + ww].astype(jnp.bfloat16)
-        g2_copy(i, m, jx).start()
-
-    def pass_on(i, last):
-        for jx in range(nx):
-            g1_copy(i, jx).wait_recv()
-            mine = block(2 * lax.rem(x + jx, nx) + core)
-            both = g[i, mine, :] + r1[i, jx]
-            for m in range(q):
-                if last and jx == 0:
-                    @pl.when(m == mm)
-                    def _():
-                        own[...] = both[:, starts[m]:starts[m] + ww]
-
-                    @pl.when(m != mm)
-                    def _():
-                        send_block(i, m, jx, both)
-                else:
-                    send_block(i, m, jx, both)
+    def pair_sum(i, jx):
+        g1_copy(i, jx).wait_recv()
+        return g[i, block(2 * lax.rem(x + jx, nx) + core), :] + r1[i, jx]
+
+    def to_x(i):
+        for jx in range(1, nx):
+            sx[i, jx - 1] = pair_sum(i, jx).astype(jnp.bfloat16)
+            gx_copy(i, jx).start()
+
+    def to_vocab(i, last):
+        both = pair_sum(i, 0)
+        for jx in range(1, nx):
+            gx_copy(i, jx).wait_recv()
+            both += rx[i, jx - 1].astype(jnp.float32)
+        for m in range(q):
+            def send_block():
+                s2[i, m] = both[:, starts[m]:starts[m] + ww].astype(jnp.bfloat16)
+                g2_copy(i, m).start()
+
+            if last:
+                @pl.when(m == mm)
+                def _():
+                    own[...] = both[:, starts[m]:starts[m] + ww]
+
+                pl.when(m != mm)(send_block)
+            else:
+                send_block()
 
     def second(i, _):
         part = pl.ds(pl.multiple_of(lax.rem(mg + 1 + i, ng) * group, group), group)
@@ -281,35 +301,45 @@
 
         @pl.when(i > 0)
         def _():
-            pass_on(i - 1, False)
+            to_x(i - 1)
+
+        @pl.when(i > 1)
+        def _():
+            to_vocab(i - 2, False)
 
         return 0
 
     lax.fori_loop(0, ng, second, 0)
-    pass_on(ng - 1, True)
-
-    def not_own(i, m, jx):
-        return (m != mm) if (i == ng - 1 and jx == 0) else (mm >= 0)
+    to_x(ng - 1)
+    if ng > 1:
+        to_vocab(ng - 2, False)
+    to_vocab(ng - 1, True)
+
+    def not_own(i, m):
+        return (m != mm) if i == ng - 1 else (mm >= 0)
 
     mine = block(d)
     lane = lax.broadcasted_iota(jnp.int32, (rows, 128), 1)
-    probs = jnp.where(lane >= 64, tp_all[mine, :], 1.0)
+    probs = jnp.where(lane >= top_n, tp_all[mine, :], 1.0)
     entropy = jnp.sum(probs * jnp.log(probs), axis=1, keepdims=True)
-    mass = jnp.sum(jnp.where(lane >= 64, probs, 0.0), axis=1, keepdims=True)
-    div_out[...] = entropy - cols2[mine, 1:2] + mass * cols2[mine, 0:1]
+    mass = jnp.sum(jnp.where(lane >= top_n, probs, 0.0), axis=1, keepdims=True)
+    diagonal = lax.broadcasted_iota(jnp.int32, (rows, rows), 0) == (
+        lax.broadcasted_iota(jnp.int32, (rows, rows), 1))
+    column = entropy - cols2[mine, 1:2] + mass * cols2[mine, 0:1]
+    div_out[...] = jnp.sum(jnp.where(diagonal, column, 0.0), axis=0, keepdims=True)
+    weight = jnp.sum(jnp.where(diagonal, tw[...], 0.0), axis=1, keepdims=True)
 
     for i in range(ng):
-        for jx in range(nx):
-            for m in range(q):
-                @pl.when(not_own(i, m, jx))
-                def _():
-                    g2_in(i, m, jx).wait_recv()
-                    own[...] += r2[i, m, jx].astype(jnp.float32)
+        for m in range(q):
+            @pl.when(not_own(i, m))
+            def _():
+                g2_in(i, m).wait_recv()
+                own[...] += r2[i, m].astype(jnp.float32)
     for m in range(q):
         @pl.when(m == mm)
         def _():
             lo = m * feat - starts[m]
-            grad_out[...] = own[:, lo:lo + feat] * tw[...]
+            grad_out[...] = own[:, lo:lo + feat] * weight
 
     for c in range(nk):
         for j in range(1, nx):
@@ -323,10 +353,12 @@
     for i in range(ng):
         for jx in range(nx):
             g1_copy(i, jx).wait_send()
-            for m in range(q):
-                @pl.when(not_own(i, m, jx))
-                def _():
-                    g2_copy(i, m, jx).wait_send()
+        for jx in range(1, nx):
+            gx_copy(i, jx).wait_send()
+        for m in range(q):
+            @pl.when(not_own(i, m))
+            def _():
+                g2_copy(i, m).wait_send()
 
 
 def body(ndp, nv, hidden, head_weight, teacher_ids, teacher_probs, token_weight):
@@ -340,34 +372,35 @@
     nt = (cols_n + 127) // 128
     na = (nt + 7) // 8 * 8
     srows = (3 * (tok // 128) + 7) // 8 * 8
-    tp = jnp.concatenate([teacher_ids.astype(jnp.float32), teacher_probs], axis=1)
     f32, bf16, dma = jnp.float32, jnp.bfloat16, pltpu.SemaphoreType.DMA
     anyspace = pl.BlockSpec(memory_space=pl.ANY)
     vmem = pl.BlockSpec(memory_space=pltpu.VMEM)
     div, out = pl.pallas_call(
         functools.partial(kernel, ndp, nv, kc),
         out_shape=(
-            jax.ShapeDtypeStruct((rows, 1), f32), jax.ShapeDtypeStruct((rows, feat), f32)),
-        in_specs=[anyspace, anyspace, vmem, vmem],
+            jax.ShapeDtypeStruct((1, rows), f32), jax.ShapeDtypeStruct((rows, feat), f32)),
+        in_specs=[anyspace, anyspace, vmem, vmem, vmem],
         out_specs=(vmem, vmem),
         scratch_shapes=[
             pltpu.VMEM((cols_n, depth), bf16), pltpu.VMEM((tok, depth), bf16),
             pltpu.VMEM((tok, 128), f32), pltpu.VMEM((na * tok, 128), f32),
             pltpu.VMEM((tok, nt * 128), f32), pltpu.VMEM((tok, cols_n), bf16),
             pltpu.VMEM((ng, tok, group), f32), pltpu.VMEM((ng, nx, rows, group), f32),
-            pltpu.VMEM((ng, q, nx, rows, ww), bf16), pltpu.VMEM((ng, q, nx, rows, ww), bf16),
+            pltpu.VMEM((ng, nx - 1, rows, group), bf16),
+            pltpu.VMEM((ng, nx - 1, rows, group), bf16),
+            pltpu.VMEM((ng, q, rows, ww), bf16), pltpu.VMEM((ng, q, rows, ww), bf16),
             pltpu.VMEM((nd, srows, 128), f32), pltpu.VMEM((tok, 128), f32),
             pltpu.VMEM((tok, 128), f32), pltpu.VMEM((128, tok), f32),
             pltpu.VMEM((rows, ww), f32),
             dma((nk,)), dma((1,)), dma((nx - 1, nk)), dma((nx - 1, nk)),
             dma((nx, nk)), dma((nx, nk)), dma((ndp - 1,)), dma((ndp - 1,)),
             dma((nd - 1,)), dma((nd - 1,)), dma((ng, nx)), dma((ng, nx)),
-            dma((ng, q, nx)), dma((ng, q, nx)),
+            dma((ng, nx - 1)), dma((ng, nx - 1)), dma((ng, q)), dma((ng, q)),
         ],
         compiler_params=pltpu.CompilerParams(
             collective_id=0, has_side_effects=True, vmem_limit_bytes=67043328),
-    )(hidden, head_weight.T, tp, token_weight[:, None])
-    return div[:, 0], out
+    )(hidden, head_weight.T, teacher_ids, teacher_probs, token_weight[None, :])
+    return div[0], out
 
 
 def solution(mesh):

time: 87.3 us -> 73.4 us (0.84)
  the two profiles are of different devices: /device:TPU:13 before, /device:TPU:0 now
where the time goes in v2:
time: 73.4 us; the launch traced here: 73.2 us
  Pallas kernels  69.8 us (95%)
  local copies, waits for them, and re-layouts  2.74 us (4%)
    pallas_call x1, Pallas kernels, body(): pl.pallas_call(functools.partial(kernel, ndp, nv, kc), out_shape=(jax.Sha...  69.8 us
    unnamed x2, local copies, waits for them, and re-layouts  2.74 us

profile of v2, /device:TPU:0, one launch (start us, length us, event | category | flops | bytes accessed | tf_op | source)
XLA Modules:
  0.0 73.2 jit_solution(17403787428273358504)
XLA Ops:
  0.6 69.8 %shard_map.68 = (f32[1,64]{1,0:T(1,128)}, f32[64,448]{1,0:T(8,128)}) custom-call(bf16[64,3584]{1,0:T(8,128)(2,1)} %hid.1, bf16[4752,3584]{1,0:T(8,128)(2,1)} %bitcast.3, s32[64,64]{1,0:T(8,128)} %ids_in.1, f32[64,64]{1,0:T(8,128)} %probs_in.1, f32[1,64]{1,0:T(1,128)} %bitcast.4), custom_call_target="tpu_custom_call" | custom-call | tf_op jit(solution)/shard_map/pallas_call | solution.py:378
  70.4 1.2 %copy.9 = f32[64]{0:T(128)} copy(f32[64]{0:T(128)} %bitcast.5) | data formatting | bytes 512
  71.6 1.6 %copy.10 = f32[64,448]{1,0:T(8,128)} copy(f32[64,448]{1,0:T(8,128)} %get-tuple-element.9) | data formatting | bytes 229376
